TPU v7x, 32 devices: a whole 2x2x4 slice. The times are simulated.
32 devices in a mesh: parts: 2 (over y), tok: 4 (over z), hid: 4 (over x, core).
Axes of the slice: x: 2, y: 2, z: 4, core: 2. Of those that a mesh axis runs over, the one named last changes fastest.
Arguments:
- tokens: bfloat16 [6144, 8192], P(('parts', 'tok'), 'hid'), parts along dimension 0, may hold values from -6 to 6
- adapter_ids: int32 [6144, 1], P(('parts', 'tok')), parts along dimension 0, may hold values from 0 to 31; in each aligned block of 768 rows (0 to 767, 768 to 1535, ...) at most 72 rows name the same one
- value_weight: bfloat16 [8192, 1024], P('hid'), may hold values from -0.0625 to 0.0625
- adapter_down: bfloat16 [32, 16, 8192], P('tok', None, 'hid'), may hold values from -0.0625 to 0.0625
- adapter_up: bfloat16 [32, 16, 1024], P('tok', None, 'hid'), may hold values from -1.5 to 1.5
Outputs:
- value_out: bfloat16 [6144, 1024], P(('parts', 'tok'), 'hid'), parts along dimension 0
There are 2 independent parts, one for each index of `parts`. A program takes and returns all parts, laid end to end along the dimension named above; an argument that names none is the same for every part. Nothing has to cross between parts.
Inputs may be any that keep to these rules, and one draw needn't show every extreme that they name: `adapter_ids`: among the 768 tokens of one index of tok, each adapter id appears at most 72 times; in some of these aligned blocks one id appears exactly 72 times.
All inputs are finite; a program needn't handle non-finite values.
Results may differ from a plain program's by a relative error of at most 0.0048.
Values may be sent and summed in bfloat16 or wider, within the bound.
A program may use at most 128 MiB of HBM per device.

v0:
```python
import functools

import jax
import jax.numpy as jnp
from jax import lax
from jax.experimental import pallas as pl
from jax.experimental.pallas import tpu as pltpu
from jax.sharding import PartitionSpec as P

MESH = pl.DeviceIdType.MESH
F32 = jnp.float32
BF16 = jnp.bfloat16


def kernel(
    n_tok,
    n_hid,
    pieces,
    extra,
    rank,
    ids_ref,
    tokens_hbm,
    value_hbm,
    down_hbm,
    up_hbm,
    out_ref,
    tokens,
    value,
    adapters,
    core_send,
    core_recv,
    partial,
    chip_send,
    chip_recv,
    picked,
    wanted,
    low_send,
    low_recv,
    load_sem,
    right_sem,
    left_sem,
    line_sem,
    pair_send_sem,
    pair_recv_sem,
    core_send_sem,
    core_recv_sem,
    chip_send_sem,
    chip_recv_sem,
    low_send_sem,
    low_recv_sem,
):
    y = lax.axis_index("parts")
    z = lax.axis_index("tok")
    h = lax.axis_index("hid")
    chips = n_hid // 2
    core = lax.rem(h, 2)
    x = lax.div(h, 2)
    rows, depth = tokens.shape
    kv = out_ref.shape[1]
    lanes = adapters.shape[1]
    adp_dev = lanes // rank
    half = lanes // 2
    piece = half // pieces

    load_down = pltpu.make_async_copy(down_hbm, adapters.at[z, :, pl.ds(0, depth)], load_sem.at[0])
    load_up = pltpu.make_async_copy(up_hbm, adapters.at[z, :, pl.ds(depth, kv)], load_sem.at[1])
    load_tokens = pltpu.make_async_copy(tokens_hbm, tokens, load_sem.at[2])
    load_value = pltpu.make_async_copy(value_hbm, value, load_sem.at[3])
    load_down.start()
    load_up.start()

    barrier = pltpu.get_barrier_semaphore()
    pl.semaphore_signal(barrier, inc=1, device_id={"parts": 1 - y}, device_id_type=MESH)
    for d in range(1, n_hid):
        pl.semaphore_signal(
            barrier, inc=1, device_id={"hid": lax.rem(h + d, n_hid)}, device_id_type=MESH
        )

    @pl.when(z > 0)
    def _():
        pl.semaphore_signal(barrier, inc=1, device_id={"tok": z - 1}, device_id_type=MESH)

    @pl.when(z < n_tok - 1)
    def _():
        pl.semaphore_signal(barrier, inc=1, device_id={"tok": z + 1}, device_id_type=MESH)

    load_down.wait()
    load_up.wait()
    load_tokens.start()
    load_value.start()

    neighbours = (z > 0).astype(jnp.int32) + (z < n_tok - 1).astype(jnp.int32)
    pl.semaphore_wait(barrier, n_hid + neighbours)

    def chunk(block, side, c):
        start = pl.multiple_of(side * half + c * piece, piece)
        return adapters.at[block, pl.ds(start, piece)]

    def line_chunk(block, c):
        return chunk(block, y, c) if c < pieces else chunk(block, 1 - y, c - extra)

    def to_right(block, c):
        ref = line_chunk(block, c)
        return pltpu.make_async_remote_copy(
            src_ref=ref,
            dst_ref=ref,
            send_sem=right_sem.at[block, c],
            recv_sem=line_sem.at[block, c],
            device_id={"tok": z + 1},
            device_id_type=MESH,
        )

    def to_left(block, c):
        ref = line_chunk(block, c)
        return pltpu.make_async_remote_copy(
            src_ref=ref,
            dst_ref=ref,
            send_sem=left_sem.at[block, c],
            recv_sem=line_sem.at[block, c],
            device_id={"tok": z - 1},
            device_id_type=MESH,
        )

    def to_pair(block, side, c):
        ref = chunk(block, side, c)
        return pltpu.make_async_remote_copy(
            src_ref=ref,
            dst_ref=ref,
            send_sem=pair_send_sem.at[block, c],
            recv_sem=pair_recv_sem.at[block, c],
            device_id={"parts": 1 - y},
            device_id_type=MESH,
        )

    for c in range(pieces):
        @pl.when(z < n_tok - 1)
        def _():
            to_right(z, c).start()

        @pl.when(z > 0)
        def _():
            to_left(z, c).start()

    for c in range(pieces, pieces + extra):
        @pl.when(z == 0)
        def _():
            to_right(z, c).start()

        @pl.when(z == n_tok - 1)
        def _():
            to_left(z, c).start()

    def by_pair(block, c):
        return c < pieces - extra or (block != 0) & (block != n_tok - 1)

    def forward(s, first, last):
        from_left = z - 1 - s
        from_right = z + 1 + s
        for c in range(first, last):
            @pl.when(from_left >= 0 if c < pieces else from_left == 0)
            def _():
                to_right(from_left, c).wait_recv()

                @pl.when(z < n_tok - 1)
                def _():
                    to_right(from_left, c).start()

                if c < pieces:
                    @pl.when(by_pair(from_left, c))
                    def _():
                        to_pair(from_left, y, c).start()

            @pl.when(from_right < n_tok if c < pieces else from_right == n_tok - 1)
            def _():
                to_left(from_right, c).wait_recv()

                @pl.when(z > 0)
                def _():
                    to_left(from_right, c).start()

                if c < pieces:
                    @pl.when(by_pair(from_right, c))
                    def _():
                        to_pair(from_right, y, c).start()

    load_tokens.wait()
    load_value.wait()

    def base_block(j):
        columns = pl.ds(pl.multiple_of(j * kv, kv), kv)
        return jnp.dot(tokens[...], value[:, columns], preferred_element_type=F32)

    def to_core(i):
        return pltpu.make_async_remote_copy(
            src_ref=core_send.at[i],
            dst_ref=core_recv.at[i],
            send_sem=core_send_sem.at[i],
            recv_sem=core_recv_sem.at[i],
            device_id={"hid": x * 2 + 1 - core},
            device_id_type=MESH,
        )

    passed = 0
    for k in range(2 * chips):
        i = k % chips
        if k < chips:
            core_send[i] = base_block(i * 2 + 1 - core).astype(BF16)
            to_core(i).start()
        else:
            partial[i] = base_block(i * 2 + core)
        upto = pieces * (k + 1) // (2 * chips)
        forward(0, passed, upto)
        passed = upto

    forward(0, pieces, pieces + extra)

    def to_chip(i, slot):
        return pltpu.make_async_remote_copy(
            src_ref=chip_send.at[i],
            dst_ref=chip_recv.at[slot],
            send_sem=chip_send_sem.at[i],
            recv_sem=chip_recv_sem.at[slot],
            device_id={"hid": i * 2 + core},
            device_id_type=MESH,
        )

    for d in range(1, chips):
        i = lax.rem(x + d, chips)
        to_core(i).wait_recv()
        chip_send[i] = (partial[i] + core_recv[i].astype(F32)).astype(BF16)
        to_chip(i, x).start()

    lane_adapter = lax.broadcasted_iota(jnp.int32, (rows, lanes), 1) // rank
    ids = jnp.transpose(jnp.broadcast_to(ids_ref[...], (lanes, rows)))
    wanted[...] = ids - lane_adapter

    def low_block(block):
        sums = lax.dot_general(
            tokens[...],
            adapters[block, :, 0:depth],
            (((1,), (1,)), ((), ())),
            preferred_element_type=F32,
        )
        return jnp.where(wanted[...] == block * adp_dev, sums, 0.0)

    picked[...] = low_block(z)

    def low_of(s):
        for sign in (-1, 1):
            block = z + sign * (1 + s)

            @pl.when((block >= 0) & (block < n_tok))
            def _():
                for c in range(pieces):
                    @pl.when(by_pair(block, c))
                    def _():
                        to_pair(block, 1 - y, c).wait_recv()

                picked[...] += low_block(block)

    def step(s, carry):
        forward(s + 1, 0, pieces + extra)
        low_of(s)
        return carry

    lax.fori_loop(0, n_tok - 2, step, 0)

    to_core(x).wait_recv()
    partial[x] += core_recv[x].astype(F32)
    for d in range(1, chips):
        i = lax.rem(x + d, chips)
        to_chip(i, i).wait_recv()
        partial[x] += chip_recv[i].astype(F32)

    low_of(n_tok - 2)

    fold = (
        lax.rem(lax.broadcasted_iota(jnp.int32, (rank, lanes), 1), rank)
        == lax.broadcasted_iota(jnp.int32, (rank, lanes), 0)
    ).astype(F32).astype(BF16)
    low_send[...] = lax.dot_general(
        fold,
        picked[...].astype(BF16),
        (((1,), (1,)), ((), ())),
        preferred_element_type=F32,
    ).astype(BF16)

    def to_hid(d, slot):
        return pltpu.make_async_remote_copy(
            src_ref=low_send,
            dst_ref=low_recv.at[slot],
            send_sem=low_send_sem.at[d],
            recv_sem=low_recv_sem.at[slot],
            device_id={"hid": lax.rem(h + d, n_hid)},
            device_id_type=MESH,
        )

    for d in range(1, n_hid):
        to_hid(d, h).start()
    low = low_send[...].astype(F32)
    for d in range(1, n_hid):
        slot = lax.rem(h + d, n_hid)
        to_hid(d, slot).wait_recv()
        low += low_recv[slot].astype(F32)
    low = low.astype(BF16)

    spread = lax.dot_general(low, fold, (((0,), (0,)), ((), ())), preferred_element_type=F32)
    group = 4 if n_tok % 4 == 0 else 1
    delta = None
    for g in range(0, n_tok, group):
        chosen = jnp.concatenate(
            [
                jnp.where(wanted[...] == b * adp_dev, spread, 0.0).astype(BF16)
                for b in range(g, g + group)
            ],
            axis=1,
        )
        weights = adapters[g : g + group, :, depth : depth + kv].reshape(group * lanes, kv)
        term = jnp.dot(chosen, weights, preferred_element_type=F32)
        delta = term if delta is None else delta + term
    out_ref[...] = (partial[x] + delta.astype(BF16).astype(F32)).astype(BF16)

    for d in range(1, n_hid):
        to_hid(d, h).wait_send()
    for i in range(chips):
        to_core(i).wait_send()
    for d in range(1, chips):
        to_chip(lax.rem(x + d, chips), x).wait_send()

    def drain(block, carry):
        for c in range(pieces + extra):
            @pl.when((block <= z if c < pieces else block == 0) & (z < n_tok - 1))
            def _():
                to_right(block, c).wait_send()

            @pl.when((block >= z if c < pieces else block == n_tok - 1) & (z > 0))
            def _():
                to_left(block, c).wait_send()

            if c < pieces:
                @pl.when((block != z) & by_pair(block, c))
                def _():
                    to_pair(block, y, c).wait_send()

        return carry

    lax.fori_loop(0, n_tok, drain, 0)


def per_device(n_tok, n_hid, tokens, adapter_ids, value_weight, adapter_down, adapter_up):
    rows, depth = tokens.shape
    adp_dev, rank, kv = adapter_up.shape
    lanes = adp_dev * rank
    chips = n_hid // 2
    pieces = 8 if n_tok <= 8 else 1
    extra = 2 if pieces == 8 else 0
    vmem = pl.BlockSpec(memory_space=pltpu.VMEM)
    hbm = pl.BlockSpec(memory_space=pltpu.HBM)
    dma = pltpu.SemaphoreType.DMA
    return pl.pallas_call(
        functools.partial(kernel, n_tok, n_hid, pieces, extra, rank),
        out_shape=jax.ShapeDtypeStruct((rows, kv), BF16),
        in_specs=[vmem, hbm, hbm, hbm, hbm],
        out_specs=vmem,
        scratch_shapes=[
            pltpu.VMEM((rows, depth), BF16),
            pltpu.VMEM(value_weight.shape, BF16),
            pltpu.VMEM((n_tok, lanes, depth + kv), BF16),
            pltpu.VMEM((chips, rows, kv), BF16),
            pltpu.VMEM((chips, rows, kv), BF16),
            pltpu.VMEM((chips, rows, kv), F32),
            pltpu.VMEM((chips, rows, kv), BF16),
            pltpu.VMEM((chips, rows, kv), BF16),
            pltpu.VMEM((rows, lanes), F32),
            pltpu.VMEM((rows, lanes), jnp.int32),
            pltpu.VMEM((rank, rows), BF16),
            pltpu.VMEM((n_hid, rank, rows), BF16),
            dma((4,)),
            dma((n_tok, pieces + extra)),
            dma((n_tok, pieces + extra)),
            dma((n_tok, pieces + extra)),
            dma((n_tok, pieces)),
            dma((n_tok, pieces)),
            dma((chips,)),
            dma((chips,)),
            dma((chips,)),
            dma((chips,)),
            dma((n_hid,)),
            dma((n_hid,)),
        ],
        compiler_params=pltpu.CompilerParams(
            collective_id=0, has_side_effects=True, vmem_limit_bytes=60 * 1024 * 1024
        ),
    )(
        adapter_ids.reshape(1, rows),
        tokens,
        value_weight,
        adapter_down.reshape(lanes, depth),
        adapter_up.reshape(lanes, kv),
    )


def solution(mesh):
    in_specs = (
        P(("parts", "tok"), "hid"),
        P(("parts", "tok"), None),
        P("hid", None),
        P("tok", None, "hid"),
        P("tok", None, "hid"),
    )
    out_specs = P(("parts", "tok"), "hid")
    body = functools.partial(per_device, mesh.shape["tok"], mesh.shape["hid"])
    return jax.shard_map(body, mesh=mesh, in_specs=in_specs, out_specs=out_specs, check_vma=False)
```

profile of v0, /device:TPU:0, one launch (start us, length us, event | category | flops | bytes accessed | tf_op | source)
XLA Modules:
  0.0 38.3 jit_solution(12441064921199597044)
XLA Ops:
  0.0 36.5 %shard_map.55 = bf16[768,256]{1,0:T(8,128)(2,1)} custom-call(s32[1,768]{1,0:T(1,128)} %bitcast.5, bf16[768,2048]{1,0:T(8,128)(2,1)} %tokens_hbm.1, bf16[2048,1024]{1,0:T(8,128)(2,1)} %value_hbm.1, bf16[128,2048]{1,0:T(8,128)(2,1)} %bitcast.3, bf16[128,256]{1,0:T(8,128)(2,1)} %bitcast.4), custom_call_target="tpu_custom_call" | custom-call | tf_op jit(solution)/shard_map/pallas_call | solution.py:360
  36.5 1.8 %copy.7 = bf16[768,256]{1,0:T(8,128)(2,1)} copy(bf16[768,256]{1,0:T(8,128)(2,1)} %shard_map.55) | data formatting | bytes 786432
where the time goes:
time: 38.5 us; the launch traced here: 38.3 us
  Pallas kernels  36.5 us (95%)
  local copies, waits for them, and re-layouts  1.77 us (5%)
    pallas_call x1, Pallas kernels, per_device(): pl.pallas_call(functools.partial(kernel, n_tok, n_hid, pieces, extra, ran...  36.5 us
    unnamed x1, local copies, waits for them, and re-layouts  1.77 us

commit v1 on v0

v1 whole, which is shorter than its diff:
```python
import functools

import jax
import jax.numpy as jnp
from jax import lax
from jax.experimental import pallas as pl
from jax.experimental.pallas import tpu as pltpu
from jax.sharding import PartitionSpec as P

MESH = pl.DeviceIdType.MESH
F32 = jnp.float32
BF16 = jnp.bfloat16

CHUNKS = 4
SPLIT = 2
PIECES = CHUNKS * SPLIT
EXTRA = SPLIT
UP = PIECES + EXTRA


def kernel(
    n_tok,
    n_hid,
    rank,
    ids_hbm,
    tokens_hbm,
    value_hbm,
    down_hbm,
    up_hbm,
    out_ref,
    ids,
    tokens,
    value,
    downs,
    ups,
    core_send,
    core_recv,
    partial,
    chip_send,
    chip_recv,
    picked,
    wanted,
    low_send,
    low_recv,
    load_sem,
    right_sem,
    left_sem,
    line_sem,
    extra_sem,
    pair_send_sem,
    pair_recv_sem,
    core_send_sem,
    core_recv_sem,
    chip_send_sem,
    chip_recv_sem,
    low_send_sem,
    low_recv_sem,
    ready_sem,
):
    y = lax.axis_index("parts")
    z = lax.axis_index("tok")
    h = lax.axis_index("hid")
    chips = n_hid // 2
    core = lax.rem(h, 2)
    x = lax.div(h, 2)
    rows, depth = tokens.shape
    kv = out_ref.shape[1]
    lanes, width = downs.shape[2:]
    adp_dev = lanes // rank
    part = lanes // SPLIT
    last = n_tok - 1

    load_down = [
        pltpu.make_async_copy(
            down_hbm.at[:, pl.ds(p * width, width)], downs.at[z, p], load_sem.at[3]
        )
        for p in range(2 * CHUNKS)
    ]
    chip_of = [lax.rem(x + d, chips) for d in range(chips)]
    order = [*range(1, chips), 0]
    columns_of = [(d, side) for d in order for side in (1, 0)]
    load_value = [
        pltpu.make_async_copy(
            value_hbm.at[
                :,
                pl.ds(
                    pl.multiple_of((chip_of[d] * 2 + (1 - core if side else core)) * kv, kv), kv
                ),
            ],
            value.at[k],
            load_sem.at[4],
        )
        for k, (d, side) in enumerate(columns_of)
    ]
    load_up = pltpu.make_async_copy(up_hbm, ups.at[z], load_sem.at[0])
    load_ids = pltpu.make_async_copy(ids_hbm, ids, load_sem.at[1])
    load_tokens = pltpu.make_async_copy(tokens_hbm, tokens, load_sem.at[2])
    for load in load_down:
        load.start()

    barrier = pltpu.get_barrier_semaphore()
    pl.semaphore_signal(barrier, inc=1, device_id={"parts": 1 - y}, device_id_type=MESH)
    for d in range(1, n_hid):
        pl.semaphore_signal(
            barrier, inc=1, device_id={"hid": lax.rem(h + d, n_hid)}, device_id_type=MESH
        )

    @pl.when(z < last)
    def _():
        pl.semaphore_signal(barrier, inc=1, device_id={"tok": z + 1}, device_id_type=MESH)

    pltpu.make_async_copy(downs.at[z], downs.at[z], load_sem.at[3]).wait()
    load_tokens.start()
    for load in load_value:
        load.start()
    load_up.start()
    load_ids.start()

    pl.semaphore_wait(barrier, n_hid + (z > 0).astype(jnp.int32))

    def piece(block, side, c):
        return downs.at[block, side * CHUNKS + c // SPLIT, pl.ds(c % SPLIT * part, part)]

    def line_piece(block, c):
        if c == UP:
            return ups.at[block]
        return piece(block, y, c) if c < PIECES else piece(block, 1 - y, c - EXTRA)

    def send_index(block, c):
        if c == UP:
            return n_tok + block
        return block if c < PIECES else 2 * n_tok

    def recv_sem(block, side, c):
        if PIECES <= c < UP:
            return extra_sem.at[side, c - PIECES]
        return line_sem.at[block - side, min(c, PIECES)]

    def to_right(block, c, ref=None):
        ref = line_piece(block, c) if ref is None else ref
        return pltpu.make_async_remote_copy(
            src_ref=ref,
            dst_ref=ref,
            send_sem=right_sem.at[send_index(block, c)],
            recv_sem=recv_sem(block, 0, c),
            device_id={"tok": z + 1},
            device_id_type=MESH,
        )

    def to_left(block, c, ref=None):
        ref = line_piece(block, c) if ref is None else ref
        return pltpu.make_async_remote_copy(
            src_ref=ref,
            dst_ref=ref,
            send_sem=left_sem.at[send_index(block, c)],
            recv_sem=recv_sem(block, 1, c),
            device_id={"tok": z - 1},
            device_id_type=MESH,
        )

    def to_pair(block, side, c, ref=None):
        ref = piece(block, side, c) if ref is None else ref
        return pltpu.make_async_remote_copy(
            src_ref=ref,
            dst_ref=ref,
            send_sem=pair_send_sem.at[block],
            recv_sem=pair_recv_sem.at[block - (block > z).astype(jnp.int32), c // SPLIT],
            device_id={"parts": 1 - y},
            device_id_type=MESH,
        )

    def wait_pair(block, c):
        @pl.when(by_pair(block, c * SPLIT))
        def _():
            ref = downs.at[block, (1 - y) * CHUNKS + c]
            to_pair(block, 1 - y, c * SPLIT, ref).wait_recv()

    @pl.when(z > 0)
    def _():
        pl.semaphore_signal(ready_sem, inc=1, device_id={"tok": z - 1}, device_id_type=MESH)
        for c in range(PIECES):
            to_left(z, c).start()

    @pl.when(z == last)
    def _():
        for c in range(PIECES, PIECES + EXTRA):
            to_left(z, c).start()

    def send_right():
        pl.semaphore_wait(ready_sem, 1)
        for c in range(PIECES):
            to_right(z, c).start()

        @pl.when(z == 0)
        def _():
            for c in range(PIECES, PIECES + EXTRA):
                to_right(z, c).start()

    def by_pair(block, c):
        return c < PIECES - EXTRA or (block != 0) & (block != last)

    def forward(s, first, end):
        from_left = z - 1 - s
        from_right = z + 1 + s
        for c in range(first, end):
            @pl.when(from_left >= 0 if c < PIECES else from_left == 0)
            def _():
                to_right(from_left, c).wait_recv()

                @pl.when(z < last)
                def _():
                    to_right(from_left, c).start()

                if c < PIECES:
                    @pl.when(by_pair(from_left, c))
                    def _():
                        to_pair(from_left, y, c).start()

            @pl.when(from_right <= last if c < PIECES else from_right == last)
            def _():
                to_left(from_right, c).wait_recv()

                @pl.when(z > 0)
                def _():
                    to_left(from_right, c).start()

                if c < PIECES:
                    @pl.when(by_pair(from_right, c))
                    def _():
                        to_pair(from_right, y, c).start()

    def forward_up(s):
        from_left = z - 1 - s
        from_right = z + 1 + s

        @pl.when((from_left >= 0) & (z < last))
        def _():
            to_right(from_left, UP).wait_recv()

            @pl.when((z < last - 1) | (s == n_tok - 3))
            def _():
                to_right(from_left, UP).start()

        @pl.when((from_right <= last) & (z > 0))
        def _():
            to_left(from_right, UP).wait_recv()

            @pl.when((z > 1) | (s == n_tok - 3))
            def _():
                to_left(from_right, UP).start()

    def flush_up():
        def send(block, carry):
            @pl.when(z == 1)
            def _():
                to_left(block, UP).start()

            @pl.when(z == last - 1)
            def _():
                to_right(block, UP).start()

            return carry

        lax.fori_loop(1, last, send, 0)

    alone = pl.when(z < n_tok)

    def base_block(k):
        return jnp.dot(tokens[...], value[k], preferred_element_type=F32)

    def to_core(d):
        return pltpu.make_async_remote_copy(
            src_ref=core_send.at[chip_of[d]],
            dst_ref=core_recv.at[chip_of[d]],
            send_sem=core_send_sem.at[d],
            recv_sem=core_recv_sem.at[d],
            device_id={"hid": x * 2 + 1 - core},
            device_id_type=MESH,
        )

    def to_chip(d, slot):
        i = chip_of[d]
        return pltpu.make_async_remote_copy(
            src_ref=chip_send.at[i],
            dst_ref=chip_recv.at[slot],
            send_sem=chip_send_sem.at[i],
            recv_sem=chip_recv_sem.at[slot],
            device_id={"hid": i * 2 + core},
            device_id_type=MESH,
        )

    pl.when((z > 0) & (z < last))(send_right)
    load_tokens.wait()
    pltpu.make_async_copy(value, value, load_sem.at[4]).wait()
    for n, d in enumerate(order):
        i = chip_of[d]

        @alone
        def _():
            core_send[i] = base_block(2 * n).astype(BF16)

        to_core(d).start()
        if n == 0:
            pl.when(z == 0)(send_right)
            load_up.wait()

            @pl.when(z > 1)
            def _():
                to_left(z, UP).start()

            @pl.when(z < last - 1)
            def _():
                to_right(z, UP).start()

        if d == 0:
            forward(0, 0, 1)

        @alone
        def _():
            partial[i] = base_block(2 * n + 1)

        if d > 0:
            to_core(d).wait_recv()
            chip_send[i] = (partial[i] + core_recv[i].astype(F32)).astype(BF16)
            to_chip(d, x).start()

    forward(0, 1, 3)

    load_ids.wait()
    lane_adapter = lax.broadcasted_iota(jnp.int32, (rows, lanes), 1) // rank
    ids_rows = jnp.transpose(jnp.broadcast_to(ids[...], (lanes, rows)))
    wanted[...] = ids_rows - lane_adapter

    def low_part(block, p):
        columns = pl.ds(pl.multiple_of(p * width, width), width)
        return lax.dot_general(
            tokens[:, columns],
            downs[block, p],
            (((1,), (1,)), ((), ())),
            preferred_element_type=F32,
        )

    def chosen_of(block, sums):
        return jnp.where(wanted[...] == block * adp_dev, sums, 0.0)

    def low_block(block):
        return lax.dot_general(
            tokens[...],
            jnp.concatenate([downs[block, p] for p in range(2 * CHUNKS)], axis=1),
            (((1,), (1,)), ((), ())),
            preferred_element_type=F32,
        )

    @alone
    def _():
        picked[...] = chosen_of(z, low_block(z))


    forward(0, 3, PIECES + EXTRA)

    def low_chunk(s, c):
        for at, block in ((last, last - 1 - s), (0, 1 + s)):
            @pl.when(z == at)
            def _():
                wait_pair(block, c)
                sums = low_part(block, y * CHUNKS + c) + low_part(block, (1 - y) * CHUNKS + c)
                picked[...] += chosen_of(block, sums)

    def low_whole(block, carry):
        @pl.when(block != z)
        def _():
            for c in range(CHUNKS):
                wait_pair(block, c)

            picked[...] += chosen_of(block, low_block(block))

        return carry

    def step(s, carry=0):
        for c in range(CHUNKS):
            forward(s, c * SPLIT, (c + 1) * SPLIT)
            if c == 1:
                forward_up(s - 1)
            low_chunk(s - 1, c)
        forward(s, PIECES, PIECES + EXTRA)
        return carry

    if n_tok <= 8:
        for s in range(1, n_tok - 2):
            step(s)
    else:
        lax.fori_loop(1, n_tok - 2, step, 0)
    flush_up()

    s = n_tok - 2
    for c in range(CHUNKS):
        forward(s, c * SPLIT, (c + 1) * SPLIT)
        if c == 1:
            forward_up(s - 1)
        if c < CHUNKS - 1:
            low_chunk(s - 1, c)
        if c == CHUNKS - 2:
            low_chunk(s - 1, CHUNKS - 1)
    low_chunk(s, 0)

    to_core(0).wait_recv()
    total = partial[x] + core_recv[x].astype(F32)
    for d in range(1, chips):
        to_chip(d, chip_of[d]).wait_recv()
        total += chip_recv[chip_of[d]].astype(F32)
    partial[x] = total

    forward(s, PIECES, PIECES + EXTRA)
    for c in range(1, CHUNKS - 2):
        low_chunk(s, c)
    low_chunk(s, CHUNKS - 1)
    low_chunk(s, CHUNKS - 2)

    @pl.when((z > 0) & (z < last))
    def _():
        lax.fori_loop(0, n_tok, low_whole, 0)

    fold = (
        lax.rem(lax.broadcasted_iota(jnp.int32, (rank, lanes), 1), rank)
        == lax.broadcasted_iota(jnp.int32, (rank, lanes), 0)
    ).astype(F32).astype(BF16)
    low_send[...] = lax.dot_general(
        fold,
        picked[...].astype(BF16),
        (((1,), (1,)), ((), ())),
        preferred_element_type=F32,
    ).astype(BF16)

    def to_hid(d, slot, ref=None):
        return pltpu.make_async_remote_copy(
            src_ref=low_send if ref is None else ref,
            dst_ref=low_recv.at[slot] if ref is None else ref,
            send_sem=low_send_sem,
            recv_sem=low_recv_sem.at[slot],
            device_id={"hid": lax.rem(h + d, n_hid)},
            device_id_type=MESH,
        )

    for d in range(1, n_hid):
        to_hid(d, h).start()

    def late_up(block, carry):
        @pl.when((z == 0) & (block > 0))
        def _():
            to_left(block, UP).wait_recv()

        @pl.when((z == last) & (block < last))
        def _():
            to_right(block, UP).wait_recv()

        return carry

    lax.fori_loop(0, n_tok, late_up, 0)

    low = low_send[...].astype(F32)
    for d in range(1, n_hid):
        slot = lax.rem(h + d, n_hid)
        to_hid(d, slot).wait_recv()
        low += low_recv[slot].astype(F32)
    low = low.astype(BF16)

    spread = lax.dot_general(low, fold, (((0,), (0,)), ((), ())), preferred_element_type=F32)
    group = 4 if n_tok % 4 == 0 else 1
    delta = None
    for g in range(0, n_tok, group):
        chosen = jnp.concatenate(
            [
                jnp.where(wanted[...] == b * adp_dev, spread, 0.0).astype(BF16)
                for b in range(g, g + group)
            ],
            axis=1,
        )
        weights = ups[g : g + group].reshape(group * lanes, kv)
        term = jnp.dot(chosen, weights, preferred_element_type=F32)
        delta = term if delta is None else delta + term
    out_ref[...] = (partial[x] + delta.astype(BF16).astype(F32)).astype(BF16)

    to_hid(1, h, low_recv.at[pl.ds(0, n_hid - 1)]).wait_send()
    for d in range(chips):
        to_core(d).wait_send()
    for d in range(1, chips):
        to_chip(d, x).wait_send()

    half = downs.at[0, pl.ds(0, CHUNKS)]
    short = downs.at[0, pl.ds(0, CHUNKS - EXTRA // SPLIT)]
    single = downs.at[0, pl.ds(0, EXTRA // SPLIT)]

    @pl.when(z < last)
    def _():
        to_right(0, PIECES, single).wait_send()

    @pl.when(z > 0)
    def _():
        to_left(last, PIECES, single).wait_send()

    def drain(block, carry):
        @pl.when((block <= z) & (z < last))
        def _():
            to_right(block, 0, half).wait_send()
            to_right(block, UP).wait_send()

        @pl.when((block >= z) & (z > 0))
        def _():
            to_left(block, 0, half).wait_send()
            to_left(block, UP).wait_send()

        end = (block == 0) | (block == last)

        @pl.when((block != z) & end)
        def _():
            to_pair(block, y, 0, short).wait_send()

        @pl.when((block != z) & ~end)
        def _():
            to_pair(block, y, 0, half).wait_send()

        return carry

    lax.fori_loop(0, n_tok, drain, 0)


def per_device(n_tok, n_hid, tokens, adapter_ids, value_weight, adapter_down, adapter_up):
    rows, depth = tokens.shape
    adp_dev, rank, kv = adapter_up.shape
    lanes = adp_dev * rank
    chips = n_hid // 2
    hbm = pl.BlockSpec(memory_space=pltpu.HBM)
    dma = pltpu.SemaphoreType.DMA
    return pl.pallas_call(
        functools.partial(kernel, n_tok, n_hid, rank),
        out_shape=pltpu.VMEM((rows, kv), BF16),
        in_specs=[hbm] * 5,
        out_specs=pl.BlockSpec(memory_space=pltpu.VMEM),
        scratch_shapes=[
            pltpu.VMEM((1, rows), jnp.int32),
            pltpu.VMEM((rows, depth), BF16),
            pltpu.VMEM((2 * chips, depth, kv), BF16),
            pltpu.VMEM((n_tok, 2 * CHUNKS, lanes, depth // (2 * CHUNKS)), BF16),
            pltpu.VMEM((n_tok, lanes, kv), BF16),
            pltpu.VMEM((chips, rows, kv), BF16),
            pltpu.VMEM((chips, rows, kv), BF16),
            pltpu.VMEM((chips, rows, kv), F32),
            pltpu.VMEM((chips, rows, kv), BF16),
            pltpu.VMEM((chips, rows, kv), BF16),
            pltpu.VMEM((rows, lanes), F32),
            pltpu.VMEM((rows, lanes), jnp.int32),
            pltpu.VMEM((rank, rows), BF16),
            pltpu.VMEM((n_hid, rank, rows), BF16),
            dma((5,)),
            dma((2 * n_tok + 1,)),
            dma((2 * n_tok + 1,)),
            dma((n_tok - 1, PIECES + 1)),
            dma((2, EXTRA)),
            dma((n_tok,)),
            dma((n_tok - 1, CHUNKS)),
            dma((chips,)),
            dma((chips,)),
            dma((chips,)),
            dma((chips,)),
            dma,
            dma((n_hid,)),
            pltpu.SemaphoreType.REGULAR,
        ],
        compiler_params=pltpu.CompilerParams(
            collective_id=0, has_side_effects=True, vmem_limit_bytes=60 * 1024 * 1024
        ),
    )(
        adapter_ids.reshape(1, rows),
        tokens,
        value_weight,
        adapter_down.reshape(lanes, depth),
        adapter_up.reshape(lanes, kv),
    )


def solution(mesh):
    in_specs = (
        P(("parts", "tok"), "hid"),
        P(("parts", "tok"), None),
        P("hid", None),
        P("tok", None, "hid"),
        P("tok", None, "hid"),
    )
    out_specs = P(("parts", "tok"), "hid")
    body = functools.partial(per_device, mesh.shape["tok"], mesh.shape["hid"])
    return jax.shard_map(body, mesh=mesh, in_specs=in_specs, out_specs=out_specs, check_vma=False)
```

time: 38.5 us -> 33.7 us (0.88)
  Pallas kernels: 36.5 us -> 32.8 us
  local copies, waits for them, and re-layouts: 1.77 us -> 0.75 us
    pallas_call x1, Pallas kernels: 36.5 us -> 32.8 us  [per_device(): pl.pallas_call(functools.partial(kernel, n_tok, n_hid, rank), out_shape=p...]
    unnamed x1, local copies, waits for them, and re-layouts: 1.77 us -> 0.75 us
where the time goes in v1:
time: 33.7 us; the launch traced here: 33.6 us
  Pallas kernels  32.8 us (97%)
  local copies, waits for them, and re-layouts  0.75 us (2%)
    pallas_call x1, Pallas kernels, per_device(): pl.pallas_call(functools.partial(kernel, n_tok, n_hid, rank), out_shape=p...  32.8 us
    unnamed x1, local copies, waits for them, and re-layouts  0.75 us

profile of v1, /device:TPU:0, one launch (start us, length us, event | category | flops | bytes accessed | tf_op | source)
XLA Modules:
  0.0 33.6 jit_solution(18269036235935562409)
XLA Ops:
  0.0 32.8 %shard_map.55 = bf16[768,256]{1,0:T(8,128)(2,1)S(1)} custom-call(s32[1,768]{1,0:T(1,128)} %bitcast.5, bf16[768,2048]{1,0:T(8,128)(2,1)} %tokens_hbm.1, bf16[2048,1024]{1,0:T(8,128)(2,1)} %value_hbm.1, bf16[128,2048]{1,0:T(8,128)(2,1)} %bitcast.3, bf16[128,256]{1,0:T(8,128)(2,1)} %bitcast.4), custom_call_target="tpu_custom_call" | custom-call | tf_op jit(solution)/shard_map/pallas_call | solution.py:534
  32.8 0.7 %copy.7 = bf16[768,256]{1,0:T(8,128)(2,1)} copy(bf16[768,256]{1,0:T(8,128)(2,1)S(1)} %shard_map.55) | data formatting | bytes 786432

commit v2 on v1

--- a/solution.py
+++ b/solution.py
@@ -14,7 +14,7 @@
 CHUNKS = 4
 SPLIT = 2
 PIECES = CHUNKS * SPLIT
-EXTRA = SPLIT
+EXTRA = 2
 UP = PIECES + EXTRA
 
 
@@ -38,6 +38,7 @@
     partial,
     chip_send,
     chip_recv,
+    spare,
     picked,
     wanted,
     low_send,
@@ -88,7 +89,7 @@
                 ),
             ],
             value.at[k],
-            load_sem.at[4],
+            load_sem.at[4 if k < 2 * (chips - 1) else 5],
         )
         for k, (d, side) in enumerate(columns_of)
     ]
@@ -170,10 +171,17 @@
         )
 
     def wait_pair(block, c):
-        @pl.when(by_pair(block, c * SPLIT))
-        def _():
-            ref = downs.at[block, (1 - y) * CHUNKS + c]
+        count = [by_pair(0, k) is True for k in range(c * SPLIT, (c + 1) * SPLIT)].count(True)
+        ref = downs.at[block, (1 - y) * CHUNKS + c]
+
+        @pl.when((block != 0) & (block != last))
+        def _():
             to_pair(block, 1 - y, c * SPLIT, ref).wait_recv()
+
+        if count:
+            @pl.when((block == 0) | (block == last))
+            def _():
+                to_pair(block, 1 - y, c * SPLIT, ref.at[pl.ds(0, count * part)]).wait_recv()
 
     @pl.when(z > 0)
     def _():
@@ -291,8 +299,9 @@
 
     pl.when((z > 0) & (z < last))(send_right)
     load_tokens.wait()
-    pltpu.make_async_copy(value, value, load_sem.at[4]).wait()
-    for n, d in enumerate(order):
+    others = value.at[pl.ds(0, 2 * (chips - 1))]
+    pltpu.make_async_copy(others, others, load_sem.at[4]).wait()
+    for n, d in enumerate(order[:-1]):
         i = chip_of[d]
 
         @alone
@@ -312,20 +321,16 @@
             def _():
                 to_right(z, UP).start()
 
-        if d == 0:
-            forward(0, 0, 1)
-
         @alone
         def _():
             partial[i] = base_block(2 * n + 1)
 
-        if d > 0:
-            to_core(d).wait_recv()
-            chip_send[i] = (partial[i] + core_recv[i].astype(F32)).astype(BF16)
-            to_chip(d, x).start()
-
-    forward(0, 1, 3)
-
+        to_core(d).wait_recv()
+        chip_send[i] = (partial[i] + core_recv[i].astype(F32)).astype(BF16)
+        to_chip(d, x).start()
+
+    mine = value.at[pl.ds(2 * (chips - 1), 2)]
+    pltpu.make_async_copy(mine, mine, load_sem.at[5]).wait()
     load_ids.wait()
     lane_adapter = lax.broadcasted_iota(jnp.int32, (rows, lanes), 1) // rank
     ids_rows = jnp.transpose(jnp.broadcast_to(ids[...], (lanes, rows)))
@@ -351,12 +356,43 @@
             preferred_element_type=F32,
         )
 
-    @alone
-    def _():
-        picked[...] = chosen_of(z, low_block(z))
-
-
-    forward(0, 3, PIECES + EXTRA)
+    def base_part(k, q):
+        columns = slice(q * 2 * width, (q + 1) * 2 * width)
+        return jnp.dot(tokens[:, columns], value[k, columns, :], preferred_element_type=F32)
+
+    def pair_sum(q):
+        sums = base_part(2 * (chips - 1), q)
+        if q > 0:
+            sums += spare[...]
+        if q < CHUNKS - 1:
+            spare[...] = sums
+        else:
+            core_send[x] = sums.astype(BF16)
+
+    def own_sum(q):
+        sums = base_part(2 * chips - 1, q)
+        partial[x] = sums if q == 0 else partial[x] + sums
+
+    def own_low(q):
+        sums = low_part(z, 2 * q) + low_part(z, 2 * q + 1)
+        sums = chosen_of(z, sums)
+        picked[...] = sums if q == 0 else picked[...] + sums
+
+    work = [
+        functools.partial(part_of, q)
+        for part_of in (pair_sum, own_sum, own_low)
+        for q in range(CHUNKS)
+    ]
+    done = 0
+    for c in range(PIECES):
+        forward(0, c, c + 1)
+        upto = len(work) * (c + 1) // PIECES
+        for k in range(done, upto):
+            alone(work[k])
+            if k == CHUNKS - 1:
+                to_core(0).start()
+        done = upto
+    forward(0, PIECES, PIECES + EXTRA)
 
     def low_chunk(s, c):
         for at, block in ((last, last - 1 - s), (0, 1 + s)):
@@ -366,13 +402,16 @@
                 sums = low_part(block, y * CHUNKS + c) + low_part(block, (1 - y) * CHUNKS + c)
                 picked[...] += chosen_of(block, sums)
 
-    def low_whole(block, carry):
-        @pl.when(block != z)
-        def _():
-            for c in range(CHUNKS):
-                wait_pair(block, c)
-
-            picked[...] += chosen_of(block, low_block(block))
+    def low_whole(s, carry):
+        for sign in (-1, 1):
+            block = z + sign * (1 + s)
+
+            @pl.when((block >= 0) & (block <= last))
+            def _():
+                for c in range(CHUNKS):
+                    wait_pair(block, c)
+
+                picked[...] += chosen_of(block, low_block(block))
 
         return carry
 
@@ -418,7 +457,7 @@
 
     @pl.when((z > 0) & (z < last))
     def _():
-        lax.fori_loop(0, n_tok, low_whole, 0)
+        lax.fori_loop(0, last - 1, low_whole, 0)
 
     fold = (
         lax.rem(lax.broadcasted_iota(jnp.int32, (rank, lanes), 1), rank)
@@ -486,9 +525,9 @@
     for d in range(1, chips):
         to_chip(d, x).wait_send()
 
-    half = downs.at[0, pl.ds(0, CHUNKS)]
-    short = downs.at[0, pl.ds(0, CHUNKS - EXTRA // SPLIT)]
-    single = downs.at[0, pl.ds(0, EXTRA // SPLIT)]
+    half = downs.at[0, pl.ds(0, PIECES), pl.ds(0, part)]
+    short = downs.at[0, pl.ds(0, PIECES - EXTRA), pl.ds(0, part)]
+    single = downs.at[0, pl.ds(0, EXTRA), pl.ds(0, part)]
 
     @pl.when(z < last)
     def _():
@@ -547,11 +586,12 @@
             pltpu.VMEM((chips, rows, kv), F32),
             pltpu.VMEM((chips, rows, kv), BF16),
             pltpu.VMEM((chips, rows, kv), BF16),
+            pltpu.VMEM((rows, kv), F32),
             pltpu.VMEM((rows, lanes), F32),
             pltpu.VMEM((rows, lanes), jnp.int32),
             pltpu.VMEM((rank, rows), BF16),
             pltpu.VMEM((n_hid, rank, rows), BF16),
-            dma((5,)),
+            dma((6,)),
             dma((2 * n_tok + 1,)),
             dma((2 * n_tok + 1,)),
             dma((n_tok - 1, PIECES + 1)),

time: 33.7 us -> 32.1 us (0.953)
  Pallas kernels: 32.8 us -> 31.2 us
    pallas_call x1, Pallas kernels: 32.8 us -> 31.2 us  [per_device(): pl.pallas_call(functools.partial(kernel, n_tok, n_hid, rank), out_shape=p...]
where the time goes in v2:
time: 32.1 us; the launch traced here: 31.9 us
  Pallas kernels  31.2 us (97%)
  local copies, waits for them, and re-layouts  0.75 us (2%)
    pallas_call x1, Pallas kernels, per_device(): pl.pallas_call(functools.partial(kernel, n_tok, n_hid, rank), out_shape=p...  31.2 us
    unnamed x1, local copies, waits for them, and re-layouts  0.75 us

profile of v2, /device:TPU:0, one launch (start us, length us, event | category | flops | bytes accessed | tf_op | source)
XLA Modules:
  0.0 31.9 jit_solution(15678412366446083697)
XLA Ops:
  0.0 31.2 %shard_map.55 = bf16[768,256]{1,0:T(8,128)(2,1)S(1)} custom-call(s32[1,768]{1,0:T(1,128)} %bitcast.5, bf16[768,2048]{1,0:T(8,128)(2,1)} %tokens_hbm.1, bf16[2048,1024]{1,0:T(8,128)(2,1)} %value_hbm.1, bf16[128,2048]{1,0:T(8,128)(2,1)} %bitcast.3, bf16[128,256]{1,0:T(8,128)(2,1)} %bitcast.4), custom_call_target="tpu_custom_call" | custom-call | tf_op jit(solution)/shard_map/pallas_call | solution.py:573
  31.2 0.7 %copy.7 = bf16[768,256]{1,0:T(8,128)(2,1)} copy(bf16[768,256]{1,0:T(8,128)(2,1)S(1)} %shard_map.55) | data formatting | bytes 786432

commit v3 on v2

--- a/solution.py
+++ b/solution.py
@@ -394,13 +394,14 @@
         done = upto
     forward(0, PIECES, PIECES + EXTRA)
 
-    def low_chunk(s, c):
+    def low_chunk(s, c, sides=(0, 1)):
         for at, block in ((last, last - 1 - s), (0, 1 + s)):
             @pl.when(z == at)
             def _():
-                wait_pair(block, c)
-                sums = low_part(block, y * CHUNKS + c) + low_part(block, (1 - y) * CHUNKS + c)
-                picked[...] += chosen_of(block, sums)
+                if 1 in sides:
+                    wait_pair(block, c)
+                sums = [low_part(block, (y if side == 0 else 1 - y) * CHUNKS + c) for side in sides]
+                picked[...] += chosen_of(block, sum(sums[1:], sums[0]))
 
     def low_whole(s, carry):
         for sign in (-1, 1):
@@ -417,10 +418,12 @@
 
     def step(s, carry=0):
         for c in range(CHUNKS):
-            forward(s, c * SPLIT, (c + 1) * SPLIT)
+            forward(s, c * SPLIT, c * SPLIT + 1)
+            low_chunk(s - 1, c, (0,))
+            forward(s, c * SPLIT + 1, (c + 1) * SPLIT)
             if c == 1:
                 forward_up(s - 1)
-            low_chunk(s - 1, c)
+            low_chunk(s - 1, c, (1,))
         forward(s, PIECES, PIECES + EXTRA)
         return carry
 
@@ -433,11 +436,14 @@
 
     s = n_tok - 2
     for c in range(CHUNKS):
-        forward(s, c * SPLIT, (c + 1) * SPLIT)
+        forward(s, c * SPLIT, c * SPLIT + 1)
+        if c < CHUNKS - 1:
+            low_chunk(s - 1, c, (0,))
+        forward(s, c * SPLIT + 1, (c + 1) * SPLIT)
         if c == 1:
             forward_up(s - 1)
         if c < CHUNKS - 1:
-            low_chunk(s - 1, c)
+            low_chunk(s - 1, c, (1,))
         if c == CHUNKS - 2:
             low_chunk(s - 1, CHUNKS - 1)
     low_chunk(s, 0)
@@ -452,8 +458,9 @@
     forward(s, PIECES, PIECES + EXTRA)
     for c in range(1, CHUNKS - 2):
         low_chunk(s, c)
+    low_chunk(s, CHUNKS - 2, (0,))
     low_chunk(s, CHUNKS - 1)
-    low_chunk(s, CHUNKS - 2)
+    low_chunk(s, CHUNKS - 2, (1,))
 
     @pl.when((z > 0) & (z < last))
     def _():

time: 32.1 us -> 32.1 us (level)
  no operation moved by 1% of the time
where the time goes in v3:
time: 32.1 us; the launch traced here: 31.9 us
  Pallas kernels  31.1 us (97%)
  local copies, waits for them, and re-layouts  0.75 us (2%)
    pallas_call x1, Pallas kernels, per_device(): pl.pallas_call(functools.partial(kernel, n_tok, n_hid, rank), out_shape=p...  31.1 us
    unnamed x1, local copies, waits for them, and re-layouts  0.75 us

profile of v3, /device:TPU:0, one launch (start us, length us, event | category | flops | bytes accessed | tf_op | source)
XLA Modules:
  0.0 31.9 jit_solution(8690127493617334877)
XLA Ops:
  0.0 31.1 %shard_map.55 = bf16[768,256]{1,0:T(8,128)(2,1)S(1)} custom-call(s32[1,768]{1,0:T(1,128)} %bitcast.5, bf16[768,2048]{1,0:T(8,128)(2,1)} %tokens_hbm.1, bf16[2048,1024]{1,0:T(8,128)(2,1)} %value_hbm.1, bf16[128,2048]{1,0:T(8,128)(2,1)} %bitcast.3, bf16[128,256]{1,0:T(8,128)(2,1)} %bitcast.4), custom_call_target="tpu_custom_call" | custom-call | tf_op jit(solution)/shard_map/pallas_call | solution.py:580
  31.2 0.7 %copy.7 = bf16[768,256]{1,0:T(8,128)(2,1)} copy(bf16[768,256]{1,0:T(8,128)(2,1)S(1)} %shard_map.55) | data formatting | bytes 786432
